TPU v7x, 256 devices: a whole 4x4x8 slice. The times are simulated.
256 devices in a mesh: row: 8 (over z_lo, y), col: 32 (over z_hi, x, core).
Axes of the slice: x: 4, y: 4, z: 8 (z_hi: 4, z_lo: 2; z = z_hi * 2 + z_lo), core: 2. Of those that a mesh axis runs over, the one named last changes fastest.
Arguments:
- alignment: float32 [512, 768, 256], P('row', 'col'), may hold values from -40 to 40
- seq_mask: int32 [512], replicated, may hold values 0 or 1
- res_mask: int32 [768], replicated, may hold values 0 or 1
- attn_gain: float32 [256], replicated, may hold values from 0.5 to 1.5
- outer_product_gain: float32 [256], replicated, may hold values from 0.5 to 1.5
- w_query: bfloat16 [256, 256], replicated, may hold values from -24 to 24
- w_key: bfloat16 [256, 256], replicated, may hold values from -2 to 2
- w_value: bfloat16 [256, 256], replicated, may hold values from -0.375 to 0.375
- w_gate: bfloat16 [256, 256], replicated, may hold values from -0.375 to 0.375
- output_weight: bfloat16 [256, 256], replicated, may hold values from -0.375 to 0.375
- w_left: bfloat16 [256, 32], replicated, may hold values from -0.375 to 0.375
- w_right: bfloat16 [256, 32], replicated, may hold values from -0.375 to 0.375
- w_pair: bfloat16 [1024, 128], replicated, may hold values from -3 to 3
Outputs:
- alignment_output: float32 [512, 768, 256], P('row', 'col')
- pair_increment: float32 [768, 768, 128], P('row', 'col')
All inputs are finite; a program needn't handle non-finite values.
Results may differ from a plain program's by a relative error of at most 0.0095.
Values may be sent and summed in bfloat16 or wider, within the bound.
No kernel may reach another device: no remote copies, remote signals or barrier semaphores. Data moves between devices by JAX's collectives and lax.ppermute only.
A program may use at most 128 MiB of HBM per device.

v0:
```python
import jax
import jax.numpy as jnp
from jax import lax
from jax.sharding import PartitionSpec as P

HEADS = 8
HEAD_DIM = 32


def sent_to_all(shard, axis):
    copies = jnp.broadcast_to(shard, (lax.axis_size(axis), *shard.shape))
    return lax.all_to_all(copies, axis, split_axis=0, concat_axis=0, tiled=True)


def laid_out(blocks, dim):
    blocks = jnp.moveaxis(blocks, 0, dim)
    shape = blocks.shape
    return blocks.reshape(*shape[:dim], shape[dim] * shape[dim + 1], *shape[dim + 2 :])


def gathered_copies(shard, axis, dim):
    blocks = sent_to_all(shard, axis)
    return laid_out(blocks, dim)


def normalized_rows(values, gains):
    average = jnp.mean(values, -1, keepdims=True)
    centred = values - average
    spread = jnp.mean(centred * centred, -1, keepdims=True)
    return centred * lax.rsqrt(spread + 1e-05) * gains


def shards(
    alignment,
    seq_mask,
    res_mask,
    attn_gain,
    outer_product_gain,
    w_query,
    w_key,
    w_value,
    w_gate,
    output_weight,
    w_left,
    w_right,
    w_pair,
):
    seq_dev, res_dev, channel_width = alignment.shape
    row_count = lax.axis_size("row")
    col_count = lax.axis_size("col")
    sequence_total = seq_mask.shape[0]
    hidden = w_query.shape[1]
    query_scale = HEAD_DIM ** (-0.5)
    key_bias = jnp.where(seq_mask > 0, 0.0, -1000000000.0).astype(jnp.float32)
    normed = normalized_rows(alignment, attn_gain).astype(jnp.bfloat16)
    normed = normed.reshape(seq_dev, row_count, res_dev // row_count, channel_width)

    def column(column_parts):
        col_query, col_key, col_value, col_gate = column_parts
        heads_query = col_query.reshape(sequence_total, HEADS, HEAD_DIM)
        heads_key = col_key.reshape(sequence_total, HEADS, HEAD_DIM)
        heads_value = col_value.reshape(sequence_total, HEADS, HEAD_DIM)
        logits = (
            jnp.einsum("shd,thd->hst", heads_query, heads_key, preferred_element_type=jnp.float32)
            + key_bias[None, None, :]
        )
        weights = jax.nn.softmax(logits, axis=-1).astype(jnp.bfloat16)
        attended = jnp.einsum(
            "hst,thd->shd", weights, heads_value, preferred_element_type=jnp.float32
        ).reshape(sequence_total, hidden)
        return (jax.nn.sigmoid(col_gate) * attended).astype(jnp.bfloat16)

    tokens = lax.all_to_all(normed, "row", split_axis=1, concat_axis=0, tiled=True)[:, 0]
    residues = tokens.shape[1]
    token_rows = tokens.reshape(-1, channel_width)
    queries = (
        jnp.dot(token_rows, w_query, preferred_element_type=jnp.float32) * query_scale
    ).astype(jnp.bfloat16)
    key_rows = jnp.dot(token_rows, w_key, preferred_element_type=jnp.float32).astype(jnp.bfloat16)
    value_rows = jnp.dot(token_rows, w_value, preferred_element_type=jnp.float32).astype(
        jnp.bfloat16
    )
    gate_lin = jnp.dot(token_rows, w_gate, preferred_element_type=jnp.float32)

    def arrange(values):
        return values.reshape(sequence_total, residues, -1).transpose(1, 0, 2)

    gated_output = lax.map(
        column, (arrange(queries), arrange(key_rows), arrange(value_rows), arrange(gate_lin))
    )
    gated_output = gated_output.transpose(1, 0, 2)[:, None]
    returned_value = lax.all_to_all(gated_output, "row", split_axis=0, concat_axis=1, tiled=True)
    returned_value = returned_value.reshape(-1, hidden)
    alignment_output = alignment + jnp.dot(
        returned_value, output_weight, preferred_element_type=jnp.float32
    ).reshape(seq_dev, res_dev, channel_width)
    row_index = lax.axis_index("row")
    col_index = lax.axis_index("col")
    side_width = w_left.shape[1]
    second_normalized = (
        normalized_rows(alignment_output, outer_product_gain)
        .astype(jnp.bfloat16)
        .reshape(-1, channel_width)
    )
    own_seq = lax.dynamic_slice_in_dim(seq_mask, row_index * seq_dev, seq_dev, 0)
    own_res = lax.dynamic_slice_in_dim(res_mask, col_index * res_dev, res_dev, 0)
    side_mask = (own_seq[:, None] * own_res[None, :]).astype(jnp.float32)[:, :, None]
    left = (
        (
            jnp.dot(second_normalized, w_left, preferred_element_type=jnp.float32).reshape(
                seq_dev, res_dev, side_width
            )
            * side_mask
        )
        .astype(jnp.bfloat16)
        .reshape(seq_dev, -1)
    )
    right = (
        (
            jnp.dot(second_normalized, w_right, preferred_element_type=jnp.float32).reshape(
                seq_dev, res_dev, side_width
            )
            * side_mask
        )
        .astype(jnp.bfloat16)
        .reshape(seq_dev, -1)
    )
    pair_rows = res_dev * col_count // row_count
    contraction = (((0,), (0,)), ((), ()))
    right_all = gathered_copies(right, "row", 0)
    group = seq_dev // col_count
    right_order = (
        right_all.reshape(row_count, col_count, group, -1)
        .transpose(1, 0, 2, 3)
        .reshape(sequence_total, -1)
    )
    spread_out = lax.all_to_all(left, "col", split_axis=0, concat_axis=1, tiled=True)
    own_block = lax.all_to_all(spread_out, "row", split_axis=1, concat_axis=0, tiled=True)
    products = lax.dot_general(
        lax.all_gather(own_block, "col", axis=0, tiled=True),
        right_order,
        contraction,
        preferred_element_type=jnp.float32,
    )
    outer_sum = (
        products.reshape(pair_rows, side_width, res_dev, side_width)
        .transpose(0, 2, 1, 3)
        .reshape(-1, side_width * side_width)
        .astype(jnp.bfloat16)
    )
    projected_output = jnp.dot(outer_sum, w_pair, preferred_element_type=jnp.float32).reshape(
        pair_rows, res_dev, -1
    )
    pair_res = lax.dynamic_slice_in_dim(res_mask, row_index * pair_rows, pair_rows, 0)
    live_total = jnp.sum(seq_mask)
    count_values = jnp.maximum(live_total * pair_res[:, None] * own_res[None, :], 1).astype(
        jnp.float32
    )
    return (alignment_output, projected_output / count_values[:, :, None])


def solution(mesh):
    in_specs = (P("row", "col", None), P(), P(), P(), P(), P(), P(), P(), P(), P(), P(), P(), P())
    out_specs = (P("row", "col", None), P("row", "col", None))
    return jax.shard_map(shards, mesh=mesh, in_specs=in_specs, out_specs=out_specs, check_vma=False)
```

profile of v0, /device:TPU:5, one launch (start us, length us, event | category | flops | bytes accessed | tf_op | source)
XLA Modules:
  0.0 247.4 jit_solution(861617664489180695)
XLA Ops:
  11.4 5.5 %all-to-all-start = ((bf16[64,8,3,256]{3,0,2,1:T(8,128)(2,1)}), bf16[64,8,3,256]{3,0,2,1:T(8,128)(2,1)S(1)}, u32[]{:S(2)}, u32[]{:S(2)}) async-start(bf16[64,8,3,256]{3,0,2,1:T(8,128)(2,1)} %bitcast.5), calls=%async_computation | async-start | bytes 1572864 | tf_op jit(solution)/shard_map/all_to_all | solution.py:73
  17.0 11.5 %all-to-all-done = bf16[64,8,3,256]{3,0,2,1:T(8,128)(2,1)S(1)} async-done(((bf16[64,8,3,256]{3,0,2,1:T(8,128)(2,1)}), bf16[64,8,3,256]{3,0,2,1:T(8,128)(2,1)S(1)}, u32[]{:S(2)}, u32[]{:S(2)}) %all-to-all-start) | async-done | bytes 786464 | tf_op jit(solution)/shard_map/all_to_all | solution.py:73
  31.1 2.4 reshape_squeeze.3
  42.5 2.5 reshape.159
  46.6 2.6 %convolution_bitcast_fusion = f32[3,512,256]{2,1,0:T(8,128)} fusion(bf16[512,3,256]{2,0,1:T(8,128)(2,1)} %bitcast.103, bf16[256,256]{1,0:T(8,128)(2,1)S(1)} %copy-done.3), kind=kOutput, calls=%fused_computation.25 | convolution fusion | flops 201326592 | bytes 2490368 | tf_op jit(solution)/shard_map/dot_general | solution.py:83
  49.2 40.3 %while.10 = (s32[]{:T(128)}, bf16[3,512,256]{1,2,0:T(8,128)(2,1)}, f32[3,512,256]{2,1,0:T(8,128)}, bf16[3,512,256]{1,2,0:T(8,128)(2,1)}, bf16[3,512,256]{1,2,0:T...) while((s32[]{:T(128)}, bf16[3,512,256]{1,2,0:T(8,128)(2,1)}, ...), condition=%wide.region_5.6_spmd, body=%wide.region_2.5_spmd.sunk | while | flops 279577088 | bytes 23104096 | solution.py:88
  50.3 5.0 %fusion.43 = (f32[8,512]{1,0:T(8,128)S(1)}, f32[8,512,512]{1,2,0:T(8,128)}) fusion(f32[512]{0:T(512)S(1)} %get-tuple-element.174, bf16[512,8,32]{0,2,1:T(8,128)(2,1)S(1)} %bitcast.97, bf16[512,8,32]{0,2,1:T(8,128)(2,1)S(1)} %bitcast.96), kind=kOutput, calls=%fused_computation.46.clone.1 | convolution fusion | flops 140509696 | bytes 8931328 | tf_op jit(solution)/shard_map/while/body/eval_jaxpr/sub | solution.py:67
  56.3 4.2 %fusion.44 = f32[8,32,512]{2,1,0:T(8,128)S(1)} fusion(bf16[512,8,32]{0,2,1:T(8,128)(2,1)S(1)} %bitcast.95, f32[8,512,512]{1,2,0:T(8,128)} %get-tuple-element.150, f32[8,512]{1,0:T(8,128)S(1)} %get-tuple-element.151), kind=kOutput, calls=%fused_computation.6.clone.1 | convolution fusion | flops 138412032 | bytes 9191424 | tf_op jit(solution)/shard_map/while/body/eval_jaxpr/hst,thd->shd/dot_general | solution.py:68
  63.7 5.0 %fusion.43 = (f32[8,512]{1,0:T(8,128)S(1)}, f32[8,512,512]{1,2,0:T(8,128)}) fusion(f32[512]{0:T(512)S(1)} %get-tuple-element.174, bf16[512,8,32]{0,2,1:T(8,128)(2,1)S(1)} %bitcast.97, bf16[512,8,32]{0,2,1:T(8,128)(2,1)S(1)} %bitcast.96), kind=kOutput, calls=%fused_computation.46.clone.1 | convolution fusion | flops 140509696 | bytes 8931328 | tf_op jit(solution)/shard_map/while/body/eval_jaxpr/sub | solution.py:67
  69.7 4.2 %fusion.44 = f32[8,32,512]{2,1,0:T(8,128)S(1)} fusion(bf16[512,8,32]{0,2,1:T(8,128)(2,1)S(1)} %bitcast.95, f32[8,512,512]{1,2,0:T(8,128)} %get-tuple-element.150, f32[8,512]{1,0:T(8,128)S(1)} %get-tuple-element.151), kind=kOutput, calls=%fused_computation.6.clone.1 | convolution fusion | flops 138412032 | bytes 9191424 | tf_op jit(solution)/shard_map/while/body/eval_jaxpr/hst,thd->shd/dot_general | solution.py:68
  77.1 5.0 %fusion.43 = (f32[8,512]{1,0:T(8,128)S(1)}, f32[8,512,512]{1,2,0:T(8,128)}) fusion(f32[512]{0:T(512)S(1)} %get-tuple-element.174, bf16[512,8,32]{0,2,1:T(8,128)(2,1)S(1)} %bitcast.97, bf16[512,8,32]{0,2,1:T(8,128)(2,1)S(1)} %bitcast.96), kind=kOutput, calls=%fused_computation.46.clone.1 | convolution fusion | flops 140509696 | bytes 8931328 | tf_op jit(solution)/shard_map/while/body/eval_jaxpr/sub | solution.py:67
  83.1 4.2 %fusion.44 = f32[8,32,512]{2,1,0:T(8,128)S(1)} fusion(bf16[512,8,32]{0,2,1:T(8,128)(2,1)S(1)} %bitcast.95, f32[8,512,512]{1,2,0:T(8,128)} %get-tuple-element.150, f32[8,512]{1,0:T(8,128)S(1)} %get-tuple-element.151), kind=kOutput, calls=%fused_computation.6.clone.1 | convolution fusion | flops 138412032 | bytes 9191424 | tf_op jit(solution)/shard_map/while/body/eval_jaxpr/hst,thd->shd/dot_general | solution.py:68
  89.5 2.3 copy.104
  91.8 4.3 %all-to-all-start.1 = ((bf16[512,1,3,256]{3,2,1,0:T(4,128)(2,1)}), bf16[512,1,3,256]{3,2,1,0:T(4,128)(2,1)S(1)}, u32[]{:S(2)}, u32[]{:S(2)}) async-start(bf16[512,1,3,256]{3,2,1,0:T(4,128)(2,1)} %bitcast.102), calls=%async_computation.1 | async-start | bytes 2097152 | tf_op jit(solution)/shard_map/all_to_all | solution.py:92
  97.0 14.0 %all-to-all-done.1 = bf16[512,1,3,256]{3,2,1,0:T(4,128)(2,1)S(1)} async-done(((bf16[512,1,3,256]{3,2,1,0:T(4,128)(2,1)}), bf16[512,1,3,256]{3,2,1,0:T(4,128)(2,1)S(1)}, u32[]{:S(2)}, u32[]{:S(2)}) %all-to-all-start.1) | async-done | bytes 786464 | tf_op jit(solution)/shard_map/all_to_all | solution.py:92
  114.8 19.5 %all_to_all.70 = bf16[32,2,768]{2,1,0:T(2,128)(2,1)S(1)} all-to-all(bf16[32,2,768]{2,1,0:T(2,128)(2,1)S(1)} %all_to_all.57), channel_id=1, replica_groups=mesh['row'=8,'col'=32] {'col'}, dimensions={0} | all-to-all | bytes 196608 | tf_op jit(solution)/shard_map/all_to_all | solution.py:137
  134.3 8.1 %all_to_all.71 = bf16[2,8,3072]{2,0,1:T(2,128)(2,1)S(1)} all-to-all(bf16[2,8,3072]{2,0,1:T(2,128)(2,1)S(1)} %bitcast.112), channel_id=1, replica_groups=mesh['row'=8,'col'=32] {'row'}, dimensions={1} | all-to-all | bytes 196608 | tf_op jit(solution)/shard_map/all_to_all | solution.py:138
  145.3 3.5 %all-to-all-start.4 = ((bf16[8,64,768]{2,1,0:T(8,128)(2,1)}), bf16[8,64,768]{2,1,0:T(8,128)(2,1)S(1)}, u32[]{:S(2)}, u32[]{:S(2)}) async-start(bf16[8,64,768]{2,1,0:T(8,128)(2,1)} %broadcast_in_dim.23), calls=%async_computation.4 | async-start | bytes 1572864 | tf_op jit(solution)/shard_map/all_to_all | solution.py:12
  151.0 8.0 %all-to-all-done.4 = bf16[8,64,768]{2,1,0:T(8,128)(2,1)S(1)} async-done(((bf16[8,64,768]{2,1,0:T(8,128)(2,1)}), bf16[8,64,768]{2,1,0:T(8,128)(2,1)S(1)}, u32[]{:S(2)}, u32[]{:S(2)}) %all-to-all-start.4) | async-done | bytes 786464 | tf_op jit(solution)/shard_map/all_to_all | solution.py:12
  161.6 35.4 %all-gather.2.cloned.1.call-done = bf16[512,3072]{1,0:T(8,128)(2,1)} async-done(((bf16[16,3072]{1,0:T(8,128)(2,1)}), bf16[512,3072]{1,0:T(8,128)(2,1)}) %all-gather.2.cloned.1.call-update) | async-done | bytes 3145744 | tf_op jit(solution)/shard_map/all_gather | solution.py:140
  197.0 3.2 %copy.114 = bf16[3072,512]{1,0:T(8,128)(2,1)S(1)} copy(bf16[3072,512]{0,1:T(8,128)(2,1)} %bitcast.105) | data formatting | bytes 6291456 | tf_op jit(solution)/shard_map/dot_general | solution.py:139
  200.2 13.7 %convert_bitcast_fusion = bf16[96,24,32,32]{3,2,1,0:T(8,128)(2,1)} fusion(bf16[96,32,512,1]{2,1,3,0:T(8,128)(2,1)S(1)} %bitcast.106, bf16[24,32,512,1]{2,1,0,3:T(8,128)(2,1)} %bitcast.110), kind=kOutput, calls=%fused_computation.15 | convolution fusion | flops 2418278400 | bytes 8650752 | tf_op jit(solution)/shard_map/dot_general | solution.py:139
  213.9 20.1 %copy.120 = bf16[96,24,32,32]{0,3,2,1:T(8,128)(2,1)} copy(bf16[96,24,32,32]{3,2,1,0:T(8,128)(2,1)} %convert_bitcast_fusion) | data formatting | bytes 9437184 | tf_op jit(solution)/shard_map/convert_element_type | solution.py:149
  234.1 4.8 %convolution_divide_fusion = f32[96,24,128]{2,0,1:T(8,128)S(1)} fusion(bf16[96,24,1024]{0,2,1:T(8,128)(2,1)} %bitcast.98, f32[96,24]{0,1:T(8,128)S(1)} %maximum_convert_fusion, bf16[1024,128]{1,0:T(8,128)(2,1)S(1)} %copy-done), kind=kOutput, calls=%fused_computation.27 | convolution fusion | flops 604274688 | bytes 6169600 | tf_op jit(solution)/shard_map/dot_general | solution.py:151
  (89 shorter events, 43.7 us)
Async XLA Ops:
  7.2 226.9 %copy-start = (bf16[1024,128]{1,0:T(8,128)(2,1)S(1)}, bf16[1024,128]{1,0:T(8,128)(2,1)}, u32[]{:S(2)}) copy-start(bf16[1024,128]{1,0:T(8,128)(2,1)} %param.27) | copy-start | bytes 786436
  7.2 1.9 copy-start.1
  7.2 2.7 %copy-start.9 = (f32[256]{0:T(256)S(1)}, f32[256]{0:T(256)}, u32[]{:S(2)}) copy-start(f32[256]{0:T(256)} %param.18) | copy-start | bytes 3076
  9.9 7.0 %copy-start.8 = (s32[512]{0:T(512)S(1)}, s32[512]{0:T(512)}, u32[]{:S(2)}) copy-start(s32[512]{0:T(512)} %param.16) | copy-start | bytes 6148
  11.4 17.1 %all-to-all-start = ((bf16[64,8,3,256]{3,0,2,1:T(8,128)(2,1)}), bf16[64,8,3,256]{3,0,2,1:T(8,128)(2,1)S(1)}, u32[]{:S(2)}, u32[]{:S(2)}) async-start(bf16[64,8,3,256]{3,0,2,1:T(8,128)(2,1)} %bitcast.5), calls=%async_computation | async-start | bytes 1572864 | tf_op jit(solution)/shard_map/all_to_all | solution.py:73
  30.1 3.4 %copy-start.5 = (bf16[256,256]{1,0:T(8,128)(2,1)S(1)}, bf16[256,256]{1,0:T(8,128)(2,1)}, u32[]{:S(2)}) copy-start(bf16[256,256]{1,0:T(8,128)(2,1)} %param.22) | copy-start | bytes 393220
  33.9 3.5 %copy-start.6 = (bf16[256,256]{1,0:T(8,128)(2,1)S(1)}, bf16[256,256]{1,0:T(8,128)(2,1)}, u32[]{:S(2)}) copy-start(bf16[256,256]{1,0:T(8,128)(2,1)} %param.20) | copy-start | bytes 393220
  37.7 3.5 %copy-start.7 = (bf16[256,256]{1,0:T(8,128)(2,1)S(1)}, bf16[256,256]{1,0:T(8,128)(2,1)}, u32[]{:S(2)}) copy-start(bf16[256,256]{1,0:T(8,128)(2,1)} %param.21) | copy-start | bytes 393220
  42.5 4.1 %copy-start.3 = (bf16[256,256]{1,0:T(8,128)(2,1)S(1)}, bf16[256,256]{1,0:T(8,128)(2,1)}, u32[]{:S(2)}) copy-start(bf16[256,256]{1,0:T(8,128)(2,1)} %param.23) | copy-start | bytes 393220
  91.8 19.2 %all-to-all-start.1 = ((bf16[512,1,3,256]{3,2,1,0:T(4,128)(2,1)}), bf16[512,1,3,256]{3,2,1,0:T(4,128)(2,1)S(1)}, u32[]{:S(2)}, u32[]{:S(2)}) async-start(bf16[512,1,3,256]{3,2,1,0:T(4,128)(2,1)} %bitcast.102), calls=%async_computation.1 | async-start | bytes 2097152 | tf_op jit(solution)/shard_map/all_to_all | solution.py:92
  96.0 100.9 %all-gather.2.cloned.1.call-start = ((), (), s32[]{:S(2)}) async-start(), calls=%async_computation.5 | async-start | bytes 3244032 | tf_op jit(solution)/shard_map/all_gather | solution.py:140
  111.0 0.9 copy-start.4
  112.7 30.3 %copy-start.2 = (f32[64,24,256]{2,1,0:T(8,128)}, f32[64,24,256]{2,1,0:T(8,128)S(1)}, u32[]{:S(2)}) copy-start(f32[64,24,256]{2,1,0:T(8,128)S(1)} %get-tuple-element.100) | copy-start | bytes 4718596
  112.7 0.9 copy-start.10
  112.7 0.9 copy-start.12
  113.6 29.4 %copy-start.11 = (bf16[256,32]{0,1:T(8,128)(2,1)S(1)}, bf16[256,32]{0,1:T(8,128)(2,1)}, u32[]{:S(2)}) copy-start(bf16[256,32]{0,1:T(8,128)(2,1)} %param.26) | copy-start | bytes 49156
  145.3 13.7 %all-to-all-start.4 = ((bf16[8,64,768]{2,1,0:T(8,128)(2,1)}), bf16[8,64,768]{2,1,0:T(8,128)(2,1)S(1)}, u32[]{:S(2)}, u32[]{:S(2)}) async-start(bf16[8,64,768]{2,1,0:T(8,128)(2,1)} %broadcast_in_dim.23), calls=%async_computation.4 | async-start | bytes 1572864 | tf_op jit(solution)/shard_map/all_to_all | solution.py:12
Sparse Core Ops, SparseCore 0:
  143.2 53.7 all-gather.1
where the time goes:
time: 249 us; the launch traced here: 247 us
  waiting for transfers between devices  69 us (28%)
  local copies, waits for them, and re-layouts  60.3 us (24%)
  matrix products  53.5 us (21%)
  blocking collectives  27.5 us (11%)
  between operations  14.3 us (6%)
  starting transfers between devices  13.4 us (5%)
  other arithmetic  9.38 us (4%)
    all_gather x1, waiting for transfers between devices, shards(): lax.all_gather(own_block, 'col', axis=0, tiled=True)  35.4 us
    convert_element_type x1, local copies, waits for them, and re-layouts, shards(): outer_sum = products.reshape(pair_rows, side_width, res_dev, side_width)....  20.1 us
    all_to_all x1, blocking collectives, shards(): lax.all_to_all(left, 'col', split_axis=0, concat_axis=1, tiled=True)  19.5 us
    sub x3, matrix products, column(): weights = jax.nn.softmax(logits, axis=-1).astype(jnp.bfloat16)  15 us
    all_to_all x1, waiting for transfers between devices, shards(): lax.all_to_all(gated_output, 'row', split_axis=0, concat_axis=1, tiled=True)  14 us
    dot_general x1, matrix products, shards(): lax.dot_general(lax.all_gather(own_block, 'col', axis=0, tiled=True), rig...  13.7 us
    dot_general x3, matrix products, column(): jnp.einsum('hst,thd->shd', weights, heads_value, preferred_element_type=j...  12.7 us
    all_to_all x1, waiting for transfers between devices, shards(): lax.all_to_all(normed, 'row', split_axis=1, concat_axis=0, tiled=True)[:, 0]  11.5 us
  transfers between devices with their start and end apart: 4, of which 4 were waited for; matrix products, arithmetic and copies ran while one was open for 3% of the time, Pallas kernels for 0%

commit v1 on v0

--- a/solution.py
+++ b/solution.py
@@ -137,7 +137,9 @@
     spread_out = lax.all_to_all(left, "col", split_axis=0, concat_axis=1, tiled=True)
     own_block = lax.all_to_all(spread_out, "row", split_axis=1, concat_axis=0, tiled=True)
     products = lax.dot_general(
-        lax.all_gather(own_block, "col", axis=0, tiled=True),
+        jnp.concatenate(
+            lax.all_to_all(jnp.stack([own_block] * lax.axis_size("col")), "col", 0, 0), axis=0
+        ),
         right_order,
         contraction,
         preferred_element_type=jnp.float32,

time: 249 us -> 282 us (1.13)
  the two profiles are of different devices: /device:TPU:5 before, /device:TPU:33 now
where the time goes in v1:
time: 282 us; the launch traced here: 281 us
  waiting for transfers between devices  106 us (38%)
  local copies, waits for them, and re-layouts  67.1 us (24%)
  matrix products  54.2 us (19%)
  starting transfers between devices  22.6 us (8%)
  blocking collectives  20.9 us (7%)
  other arithmetic  9.27 us (3%)
    all_to_all x1, waiting for transfers between devices, shards(): lax.all_to_all(jnp.stack([own_block] * lax.axis_size('col')), 'col', 0, 0)  65.3 us
    all_to_all x1, blocking collectives, shards(): lax.all_to_all(left, 'col', split_axis=0, concat_axis=1, tiled=True)  20.9 us
    convert_element_type x1, local copies, waits for them, and re-layouts, shards(): outer_sum = products.reshape(pair_rows, side_width, res_dev, side_width)....  20.1 us
    sub x3, matrix products, column(): weights = jax.nn.softmax(logits, axis=-1).astype(jnp.bfloat16)  15.1 us
    dot_general x1, matrix products, shards(): lax.dot_general(jnp.concatenate(lax.all_to_all(jnp.stack([own_block] * la...  14.4 us
    all_to_all x1, waiting for transfers between devices, shards(): lax.all_to_all(gated_output, 'row', split_axis=0, concat_axis=1, tiled=True)  13.8 us
    dot_general x3, matrix products, column(): jnp.einsum('hst,thd->shd', weights, heads_value, preferred_element_type=j...  12.7 us
    all_to_all x1, waiting for transfers between devices, shards(): lax.all_to_all(normed, 'row', split_axis=1, concat_axis=0, tiled=True)[:, 0]  11.9 us
  transfers between devices with their start and end apart: 5, of which 5 were waited for; matrix products, arithmetic and copies ran while one was open for 4% of the time, Pallas kernels for 0%

profile of v1, /device:TPU:33, one launch (start us, length us, event | category | flops | bytes accessed | tf_op | source)
XLA Modules:
  0.0 280.6 jit_solution(15213163013874136830)
XLA Ops:
  4.9 5.4 %all-to-all-start = ((bf16[64,8,3,256]{3,0,2,1:T(8,128)(2,1)}), bf16[64,8,3,256]{3,0,2,1:T(8,128)(2,1)S(1)}, u32[]{:S(2)}, u32[]{:S(2)}) async-start(bf16[64,8,3,256]{3,0,2,1:T(8,128)(2,1)} %bitcast.5), calls=%async_computation | async-start | bytes 1572864 | tf_op jit(solution)/shard_map/all_to_all | solution.py:73
  10.2 11.9 %all-to-all-done = bf16[64,8,3,256]{3,0,2,1:T(8,128)(2,1)S(1)} async-done(((bf16[64,8,3,256]{3,0,2,1:T(8,128)(2,1)}), bf16[64,8,3,256]{3,0,2,1:T(8,128)(2,1)S(1)}, u32[]{:S(2)}, u32[]{:S(2)}) %all-to-all-start) | async-done | bytes 786464 | tf_op jit(solution)/shard_map/all_to_all | solution.py:73
  40.2 2.6 convolution_bitcast_fusion
  42.9 40.3 %while.10 = (s32[]{:T(128)}, bf16[3,512,256]{1,2,0:T(8,128)(2,1)}, f32[3,512,256]{2,1,0:T(8,128)}, bf16[3,512,256]{1,2,0:T(8,128)(2,1)}, bf16[3,512,256]{1,2,0:T...) while((s32[]{:T(128)}, bf16[3,512,256]{1,2,0:T(8,128)(2,1)}, ...), condition=%wide.region_5.6_spmd, body=%wide.region_2.5_spmd.sunk | while | flops 279577088 | bytes 23104096 | solution.py:88
  43.9 5.0 %fusion.43 = (f32[8,512]{1,0:T(8,128)S(1)}, f32[8,512,512]{1,2,0:T(8,128)}) fusion(f32[512]{0:T(512)S(1)} %get-tuple-element.174, bf16[512,8,32]{0,2,1:T(8,128)(2,1)S(1)} %bitcast.100, bf16[512,8,32]{0,2,1:T(8,128)(2,1)S(1)} %bitcast.99), kind=kOutput, calls=%fused_computation.46.clone.1 | convolution fusion | flops 140509696 | bytes 8931328 | tf_op jit(solution)/shard_map/while/body/eval_jaxpr/sub | solution.py:67
  49.9 4.2 %fusion.44 = f32[8,32,512]{2,1,0:T(8,128)S(1)} fusion(bf16[512,8,32]{0,2,1:T(8,128)(2,1)S(1)} %bitcast.98, f32[8,512,512]{1,2,0:T(8,128)} %get-tuple-element.150, f32[8,512]{1,0:T(8,128)S(1)} %get-tuple-element.151), kind=kOutput, calls=%fused_computation.6.clone.1 | convolution fusion | flops 138412032 | bytes 9191424 | tf_op jit(solution)/shard_map/while/body/eval_jaxpr/hst,thd->shd/dot_general | solution.py:68
  57.4 5.0 %fusion.43 = (f32[8,512]{1,0:T(8,128)S(1)}, f32[8,512,512]{1,2,0:T(8,128)}) fusion(f32[512]{0:T(512)S(1)} %get-tuple-element.174, bf16[512,8,32]{0,2,1:T(8,128)(2,1)S(1)} %bitcast.100, bf16[512,8,32]{0,2,1:T(8,128)(2,1)S(1)} %bitcast.99), kind=kOutput, calls=%fused_computation.46.clone.1 | convolution fusion | flops 140509696 | bytes 8931328 | tf_op jit(solution)/shard_map/while/body/eval_jaxpr/sub | solution.py:67
  63.4 4.2 %fusion.44 = f32[8,32,512]{2,1,0:T(8,128)S(1)} fusion(bf16[512,8,32]{0,2,1:T(8,128)(2,1)S(1)} %bitcast.98, f32[8,512,512]{1,2,0:T(8,128)} %get-tuple-element.150, f32[8,512]{1,0:T(8,128)S(1)} %get-tuple-element.151), kind=kOutput, calls=%fused_computation.6.clone.1 | convolution fusion | flops 138412032 | bytes 9191424 | tf_op jit(solution)/shard_map/while/body/eval_jaxpr/hst,thd->shd/dot_general | solution.py:68
  70.8 5.0 %fusion.43 = (f32[8,512]{1,0:T(8,128)S(1)}, f32[8,512,512]{1,2,0:T(8,128)}) fusion(f32[512]{0:T(512)S(1)} %get-tuple-element.174, bf16[512,8,32]{0,2,1:T(8,128)(2,1)S(1)} %bitcast.100, bf16[512,8,32]{0,2,1:T(8,128)(2,1)S(1)} %bitcast.99), kind=kOutput, calls=%fused_computation.46.clone.1 | convolution fusion | flops 140509696 | bytes 8931328 | tf_op jit(solution)/shard_map/while/body/eval_jaxpr/sub | solution.py:67
  76.8 4.2 %fusion.44 = f32[8,32,512]{2,1,0:T(8,128)S(1)} fusion(bf16[512,8,32]{0,2,1:T(8,128)(2,1)S(1)} %bitcast.98, f32[8,512,512]{1,2,0:T(8,128)} %get-tuple-element.150, f32[8,512]{1,0:T(8,128)S(1)} %get-tuple-element.151), kind=kOutput, calls=%fused_computation.6.clone.1 | convolution fusion | flops 138412032 | bytes 9191424 | tf_op jit(solution)/shard_map/while/body/eval_jaxpr/hst,thd->shd/dot_general | solution.py:68
  85.5 3.9 %all-to-all-start.1 = ((bf16[512,1,3,256]{3,2,1,0:T(4,128)(2,1)}), bf16[512,1,3,256]{3,2,1,0:T(4,128)(2,1)S(1)}, u32[]{:S(2)}, u32[]{:S(2)}) async-start(bf16[512,1,3,256]{3,2,1,0:T(4,128)(2,1)} %bitcast.105), calls=%async_computation.1 | async-start | bytes 2097152 | tf_op jit(solution)/shard_map/all_to_all | solution.py:92
  90.3 13.8 %all-to-all-done.1 = bf16[512,1,3,256]{3,2,1,0:T(4,128)(2,1)S(1)} async-done(((bf16[512,1,3,256]{3,2,1,0:T(4,128)(2,1)}), bf16[512,1,3,256]{3,2,1,0:T(4,128)(2,1)S(1)}, u32[]{:S(2)}, u32[]{:S(2)}) %all-to-all-start.1) | async-done | bytes 786464 | tf_op jit(solution)/shard_map/all_to_all | solution.py:92
  107.9 20.9 %all_to_all.72 = bf16[32,2,768]{2,1,0:T(2,128)(2,1)} all-to-all(bf16[32,2,768]{2,1,0:T(2,128)(2,1)S(1)} %all_to_all.58), channel_id=1, replica_groups=mesh['row'=8,'col'=32] {'col'}, dimensions={0} | all-to-all | bytes 196608 | tf_op jit(solution)/shard_map/all_to_all | solution.py:137
  128.9 4.2 %all-to-all-start.3 = ((bf16[2,8,3072]{2,0,1:T(2,128)(2,1)}), bf16[2,8,3072]{2,0,1:T(2,128)(2,1)S(1)}, u32[]{:S(2)}, u32[]{:S(2)}) async-start(bf16[2,8,3072]{2,0,1:T(2,128)(2,1)} %bitcast.23), calls=%async_computation.3 | async-start | bytes 196608 | tf_op jit(solution)/shard_map/all_to_all | solution.py:138
  134.3 2.9 %all-to-all-done.3 = bf16[2,8,3072]{2,0,1:T(2,128)(2,1)S(1)} async-done(((bf16[2,8,3072]{2,0,1:T(2,128)(2,1)}), bf16[2,8,3072]{2,0,1:T(2,128)(2,1)S(1)}, u32[]{:S(2)}, u32[]{:S(2)}) %all-to-all-start.3) | async-done | bytes 98336 | tf_op jit(solution)/shard_map/all_to_all | solution.py:138
  138.2 4.6 %all-to-all-start.5 = ((bf16[8,64,768]{2,1,0:T(8,128)(2,1)}), bf16[8,64,768]{2,1,0:T(8,128)(2,1)S(1)}, u32[]{:S(2)}, u32[]{:S(2)}) async-start(bf16[8,64,768]{2,1,0:T(8,128)(2,1)} %broadcast_in_dim.23), calls=%async_computation.5 | async-start | bytes 1572864 | tf_op jit(solution)/shard_map/all_to_all | solution.py:12
  142.8 11.9 %all-to-all-done.5 = bf16[8,64,768]{2,1,0:T(8,128)(2,1)S(1)} async-done(((bf16[8,64,768]{2,1,0:T(8,128)(2,1)}), bf16[8,64,768]{2,1,0:T(8,128)(2,1)S(1)}, u32[]{:S(2)}, u32[]{:S(2)}) %all-to-all-start.5) | async-done | bytes 786464 | tf_op jit(solution)/shard_map/all_to_all | solution.py:12
  156.7 4.5 %all-to-all-start.4 = ((bf16[32,16,3072]{2,1,0:T(8,128)(2,1)}), bf16[32,16,3072]{2,1,0:T(8,128)(2,1)S(1)}, u32[]{:S(2)}, u32[]{:S(2)}) async-start(bf16[32,16,3072]{2,1,0:T(8,128)(2,1)} %stack.5), calls=%async_computation.4 | async-start | bytes 6291456 | tf_op jit(solution)/shard_map/all_to_all | solution.py:141
  166.3 2.9 %reshape.168 = bf16[512,768]{1,0:T(8,128)(2,1)} reshape(bf16[32,8,2,768]{3,2,1,0:T(2,128)(2,1)} %copy.118) | data formatting | bytes 1572864 | tf_op jit(solution)/shard_map/reshape | solution.py:135
  171.5 65.3 %all-to-all-done.4 = bf16[32,16,3072]{2,1,0:T(8,128)(2,1)S(1)} async-done(((bf16[32,16,3072]{2,1,0:T(8,128)(2,1)}), bf16[32,16,3072]{2,1,0:T(8,128)(2,1)S(1)}, u32[]{:S(2)}, u32[]{:S(2)}) %all-to-all-start.4) | async-done | bytes 3145760 | tf_op jit(solution)/shard_map/all_to_all | solution.py:141
  236.8 2.8 copy.114
  239.6 14.4 %convert_bitcast_fusion = bf16[96,24,32,32]{3,2,1,0:T(8,128)(2,1)} fusion(bf16[96,32,512,1]{2,1,3,0:T(8,128)(2,1)} %bitcast.108, bf16[24,32,512,1]{2,1,0,3:T(8,128)(2,1)} %bitcast.112), kind=kOutput, calls=%fused_computation.15 | convolution fusion | flops 2418278400 | bytes 8650752 | tf_op jit(solution)/shard_map/dot_general | solution.py:139
  254.0 20.1 %copy.120 = bf16[96,24,32,32]{0,3,2,1:T(8,128)(2,1)} copy(bf16[96,24,32,32]{3,2,1,0:T(8,128)(2,1)} %convert_bitcast_fusion) | data formatting | bytes 9437184 | tf_op jit(solution)/shard_map/convert_element_type | solution.py:151
  274.1 4.8 %convolution_divide_fusion = f32[96,24,128]{2,0,1:T(8,128)S(1)} fusion(bf16[96,24,1024]{0,2,1:T(8,128)(2,1)} %bitcast.101, f32[96,24]{0,1:T(8,128)S(1)} %maximum_convert_fusion, bf16[1024,128]{1,0:T(8,128)(2,1)S(1)} %copy-done), kind=kOutput, calls=%fused_computation.27 | convolution fusion | flops 604274688 | bytes 6169600 | tf_op jit(solution)/shard_map/dot_general | solution.py:153
  (92 shorter events, 55.0 us)
Async XLA Ops:
  0.6 273.5 %copy-start = (bf16[1024,128]{1,0:T(8,128)(2,1)S(1)}, bf16[1024,128]{1,0:T(8,128)(2,1)}, u32[]{:S(2)}) copy-start(bf16[1024,128]{1,0:T(8,128)(2,1)} %param.27) | copy-start | bytes 786436
  0.6 1.9 copy-start.1
  0.7 2.7 copy-start.10
  3.4 6.9 %copy-start.9 = (s32[512]{0:T(512)S(1)}, s32[512]{0:T(512)}, u32[]{:S(2)}) copy-start(s32[512]{0:T(512)} %param.16) | copy-start | bytes 6148
  4.9 17.2 %all-to-all-start = ((bf16[64,8,3,256]{3,0,2,1:T(8,128)(2,1)}), bf16[64,8,3,256]{3,0,2,1:T(8,128)(2,1)S(1)}, u32[]{:S(2)}, u32[]{:S(2)}) async-start(bf16[64,8,3,256]{3,0,2,1:T(8,128)(2,1)} %bitcast.5), calls=%async_computation | async-start | bytes 1572864 | tf_op jit(solution)/shard_map/all_to_all | solution.py:73
  23.8 3.4 %copy-start.6 = (bf16[256,256]{1,0:T(8,128)(2,1)S(1)}, bf16[256,256]{1,0:T(8,128)(2,1)}, u32[]{:S(2)}) copy-start(bf16[256,256]{1,0:T(8,128)(2,1)} %param.22) | copy-start | bytes 393220
  27.5 3.5 %copy-start.7 = (bf16[256,256]{1,0:T(8,128)(2,1)S(1)}, bf16[256,256]{1,0:T(8,128)(2,1)}, u32[]{:S(2)}) copy-start(bf16[256,256]{1,0:T(8,128)(2,1)} %param.20) | copy-start | bytes 393220
  31.4 3.5 %copy-start.8 = (bf16[256,256]{1,0:T(8,128)(2,1)S(1)}, bf16[256,256]{1,0:T(8,128)(2,1)}, u32[]{:S(2)}) copy-start(bf16[256,256]{1,0:T(8,128)(2,1)} %param.21) | copy-start | bytes 393220
  36.1 4.1 %copy-start.4 = (bf16[256,256]{1,0:T(8,128)(2,1)S(1)}, bf16[256,256]{1,0:T(8,128)(2,1)}, u32[]{:S(2)}) copy-start(bf16[256,256]{1,0:T(8,128)(2,1)} %param.23) | copy-start | bytes 393220
  85.5 18.6 %all-to-all-start.1 = ((bf16[512,1,3,256]{3,2,1,0:T(4,128)(2,1)}), bf16[512,1,3,256]{3,2,1,0:T(4,128)(2,1)S(1)}, u32[]{:S(2)}, u32[]{:S(2)}) async-start(bf16[512,1,3,256]{3,2,1,0:T(4,128)(2,1)} %bitcast.105), calls=%async_computation.1 | async-start | bytes 2097152 | tf_op jit(solution)/shard_map/all_to_all | solution.py:92
  104.1 0.9 copy-start.5
  105.8 27.2 %copy-start.2 = (f32[64,24,256]{2,1,0:T(8,128)}, f32[64,24,256]{2,1,0:T(8,128)S(1)}, u32[]{:S(2)}) copy-start(f32[64,24,256]{2,1,0:T(8,128)S(1)} %get-tuple-element.100) | copy-start | bytes 4718596
  105.8 0.9 copy-start.11
  105.8 0.9 copy-start.13
  106.5 26.5 %copy-start.12 = (bf16[256,32]{0,1:T(8,128)(2,1)S(1)}, bf16[256,32]{0,1:T(8,128)(2,1)}, u32[]{:S(2)}) copy-start(bf16[256,32]{0,1:T(8,128)(2,1)} %param.26) | copy-start | bytes 49156
  128.9 8.4 %all-to-all-start.3 = ((bf16[2,8,3072]{2,0,1:T(2,128)(2,1)}), bf16[2,8,3072]{2,0,1:T(2,128)(2,1)S(1)}, u32[]{:S(2)}, u32[]{:S(2)}) async-start(bf16[2,8,3072]{2,0,1:T(2,128)(2,1)} %bitcast.23), calls=%async_computation.3 | async-start | bytes 196608 | tf_op jit(solution)/shard_map/all_to_all | solution.py:138
  138.2 16.5 %all-to-all-start.5 = ((bf16[8,64,768]{2,1,0:T(8,128)(2,1)}), bf16[8,64,768]{2,1,0:T(8,128)(2,1)S(1)}, u32[]{:S(2)}, u32[]{:S(2)}) async-start(bf16[8,64,768]{2,1,0:T(8,128)(2,1)} %broadcast_in_dim.23), calls=%async_computation.5 | async-start | bytes 1572864 | tf_op jit(solution)/shard_map/all_to_all | solution.py:12
  154.7 2.0 copy-start.3
  156.7 80.1 %all-to-all-start.4 = ((bf16[32,16,3072]{2,1,0:T(8,128)(2,1)}), bf16[32,16,3072]{2,1,0:T(8,128)(2,1)S(1)}, u32[]{:S(2)}, u32[]{:S(2)}) async-start(bf16[32,16,3072]{2,1,0:T(8,128)(2,1)} %stack.5), calls=%async_computation.4 | async-start | bytes 6291456 | tf_op jit(solution)/shard_map/all_to_all | solution.py:141
